TPU v7x, 32 devices: a whole 2x2x4 slice. The times are simulated.
32 devices in a mesh: rows: 8 (over z, y), pairs: 4 (over x, core).
Axes of the slice: x: 2, y: 2, z: 4, core: 2. Of those that a mesh axis runs over, the one named last changes fastest.
Arguments:
- matrix: float32 [16384, 2048], P('rows', 'pairs'), may hold values from -40 to 40
Outputs:
- rotated: float32 [16384, 2048], P('rows', 'pairs')
All inputs are finite; a program needn't handle non-finite values.
Results may differ from a plain program's by a relative error of at most 0.0001.
Values sent between devices are 32-bit elements; how exact they have to be, the bound alone decides.
A program may use at most 64 MiB of HBM per device.

v0:
```python
import jax
import jax.numpy as jnp
from jax import lax
from jax.sharding import PartitionSpec as P

STEPS = 2


def passed_along(value, axis, by):
    length = lax.axis_size(axis)
    pairs = [(i, i + by) for i in range(length) if 0 <= i + by < length]
    return lax.ppermute(value, axis, pairs)


def spd_solve(system, right_side):
    factor = jnp.linalg.cholesky(system)
    middle = lax.linalg.triangular_solve(factor, right_side, left_side=True, lower=True)
    return lax.linalg.triangular_solve(factor, middle, left_side=True, lower=True, transpose_a=True)


def cayley_rotation(cross_block, norms_first, norms_second, rows_all):
    precise = lax.Precision.HIGHEST
    block_cols = cross_block.shape[0]
    scale_first = lax.rsqrt(norms_first / rows_all + 1e-06)
    scale_second = lax.rsqrt(norms_second / rows_all + 1e-06)
    coupling = 0.5 * cross_block * scale_first[:, None] * scale_second[None, :] / rows_all
    identity = jnp.eye(block_cols, dtype=jnp.float32)
    first_system = identity + jnp.dot(
        coupling, coupling.T, precision=precise, preferred_element_type=jnp.float32
    )
    first_sol = spd_solve(first_system, jnp.concatenate([identity, coupling], axis=1))
    lower_sol = jnp.dot(
        coupling.T, first_sol, precision=precise, preferred_element_type=jnp.float32
    )
    upper_rows = jnp.concatenate(
        [2.0 * first_sol[:, :block_cols] - identity, 2.0 * first_sol[:, block_cols:]], axis=1
    )
    lower_rows = jnp.concatenate(
        [-2.0 * lower_sol[:, :block_cols], identity - 2.0 * lower_sol[:, block_cols:]], axis=1
    )
    return jnp.concatenate([upper_rows, lower_rows], axis=0)


def shards(matrix):
    precise = lax.Precision.HIGHEST
    block_cols = matrix.shape[1] // 2
    rows_all = matrix.shape[0] * lax.axis_size("rows")
    position = lax.axis_index("pairs")
    cycle_size = lax.axis_size("pairs")
    first_block = matrix[:, :block_cols]
    second_block = matrix[:, block_cols:]
    for turn_index in range(STEPS):
        both = jnp.concatenate([first_block, second_block], axis=1)
        cross_local = lax.dot_general(
            first_block,
            second_block,
            (((0,), (0,)), ((), ())),
            precision=precise,
            preferred_element_type=jnp.float32,
        )
        first_local = jnp.sum(first_block * first_block, axis=0)
        second_local = jnp.sum(second_block * second_block, axis=0)
        cross_block, norms_first, norms_second = lax.psum(
            (cross_local, first_local, second_local), "rows"
        )
        rotate = cayley_rotation(cross_block, norms_first, norms_second, rows_all)
        turned = jnp.dot(both, rotate, precision=precise, preferred_element_type=jnp.float32)
        first_block = turned[:, :block_cols]
        second_block = turned[:, block_cols:]
        outgoing = jnp.where(position == 0, second_block, first_block)
        from_lower = passed_along(outgoing, "pairs", 1)
        from_upper = passed_along(second_block, "pairs", -1)
        next_first = jnp.where(position == 0, first_block, from_lower)
        second_block = jnp.where(position == cycle_size - 1, first_block, from_upper)
        first_block = next_first
    return jnp.concatenate([first_block, second_block], axis=1)


def solution(mesh):
    return jax.shard_map(
        shards,
        mesh=mesh,
        in_specs=(P("rows", "pairs"),),
        out_specs=P("rows", "pairs"),
        check_vma=False,
    )
```

profile of v0, /device:TPU:1, one launch (start us, length us, event | category | flops | bytes accessed | tf_op | source)
XLA Modules:
  0.0 393.6 jit_solution(14092058196522369512)
XLA Ops:
  6.5 6.4 %fusion.4 = f32[256,256]{0,1:T(8,128)} fusion(f32[2048,512]{1,0:T(8,128)} %param.6), kind=kOutput, calls=%fused_computation.14 | convolution fusion | flops 1610612736 | bytes 4456448 | tf_op jit(solution)/shard_map/dot_general | solution.py:54
  13.0 2.5 multiply_reduce_fusion.3
  15.6 18.9 %all-reduce.2 = (f32[256]{0:T(256)S(1)}, f32[256]{0:T(256)S(1)}) all-reduce(f32[256]{0:T(256)S(1)} %get-tuple-element.41, f32[256]{0:T(256)S(1)} %get-tuple-element.40), channel_id=1, replica_groups=mesh['rows'=8,'pairs'=4] {'rows'}, use_global_device_ids=true, to_apply=%region_4.0 | all-reduce | flops 512 | bytes 4096 | tf_op jit(solution)/shard_map/psum | solution.py:63
  34.5 50.0 %all-reduce.6.cloned.1.call-done = f32[256,256]{0,1:T(8,128)} async-done(((f32[256,256]{0,1:T(8,128)}), f32[256,256]{0,1:T(8,128)}) %all-reduce.6.cloned.1.call-update) | async-done | bytes 262160 | tf_op jit(solution)/shard_map/psum | solution.py:63
  84.5 1.0 multiply_multiply_fusion.1
  86.4 11.7 %cholesky.130 = f32[128,128]{1,0:T(8,128)S(1)} custom-call(f32[128,128]{1,0:T(8,128)S(1)} %cholesky.194), custom_call_target="Cholesky" | custom-call | tf_op jit(solution)/shard_map/jit(cholesky)/cholesky | solution.py:16
  98.1 9.8 %custom-call.17 = f32[1,128,128]{1,2,0:T(8,128)S(1)} custom-call(f32[1,128,128]{2,1,0:T(8,128)S(1)} %get-tuple-element.93), custom_call_target="InvertDiagBlocksLowerTriangular" | custom-call | tf_op jit(solution)/shard_map/jit(cholesky)/cholesky | solution.py:16
  108.4 11.7 %cholesky.147 = f32[128,128]{1,0:T(8,128)S(1)} custom-call(f32[128,128]{1,0:T(8,128)S(1)} %convolution_subtract_fusion.5), custom_call_target="Cholesky" | custom-call | tf_op jit(solution)/shard_map/jit(cholesky)/cholesky | solution.py:16
  120.2 0.7 compare_reduce_fusion.2
  120.9 0.6 compare_reduce_fusion.3
  123.0 4.1 %while.8 = (s32[]{:T(128)}, f32[256,256]{1,0:T(8,128)S(1)}, s32[2,2]{1,0:T(2,128)S(1)}, f32[2,128,128]{2,1,0:T(8,128)S(1)}, s32[]{:T(128)}) while((s32[]{:T(128)}, f32[256,256]{1,0:T(8,128)S(1)}, s32[2,2]{1,0:T(2,128)S(1)}, f32[2,128,128]{2,1,0:T(8,128)S(1)}, s32[]{:T(128)}) %tuple.63), condition=%wide.while_cond.1, body=%wide.while_body.1.sunk | while | flops 2 | bytes 131181 | solution.py:18
  123.6 1.4 bitcast_dynamic-update-slice_fusion.4
  125.7 1.4 bitcast_dynamic-update-slice_fusion.4
  127.1 20.1 %custom-call.19 = f32[2,128,128]{1,2,0:T(8,128)S(1)} custom-call(f32[2,128,128]{2,1,0:T(8,128)S(1)} %get-tuple-element.37), custom_call_target="InvertDiagBlocksLowerTriangular" | custom-call | tf_op jit(solution)/shard_map/triangular_solve/custom-call.4 | solution.py:18
  150.9 8.8 %convolution_bitcast_fusion = f32[2048,512]{0,1:T(8,128)S(1)} fusion(f32[2048,512]{1,0:T(8,128)} %param.6, f32[256,256]{0,1:T(8,128)S(1)} %get-tuple-element.85, f32[256,256]{0,1:T(8,128)S(1)} %get-tuple-element.84, f32[256,256]{0,1:T(8,128)S(1)} %get-tuple-element.83, f32[256,256]{0,1:T(8,128)S(1)} %get-tuple-element.82), kind=kOutput, calls=%fused_computation.9 | convolution fusion | flops 6443237376 | bytes 9437184 | tf_op jit(solution)/shard_map/dot_general | solution.py:67
  159.8 2.4 slice_select_fusion.5
  162.2 0.8 copy-done
  163.0 5.5 %collective-permute-start = (f32[2048,256]{0,1:T(8,128)}, f32[2048,256]{0,1:T(8,128)S(1)}, u32[]{:S(2)}, u32[]{:S(2)}) collective-permute-start(f32[2048,256]{0,1:T(8,128)} %get-tuple-element.76), channel_id=1, source_target_pairs={{0,1},{1,2},{2,3},{4,5},{5,6},{6,7},{8,9},{9,10},{10,11},{12,13},{... | collective-permute-start | bytes 6291464 | tf_op jit(solution)/shard_map/ppermute | solution.py:12
  168.5 1.9 collective-permute-start.1
  170.5 21.3 %collective-permute-done = f32[2048,256]{0,1:T(8,128)S(1)} collective-permute-done((f32[2048,256]{0,1:T(8,128)}, f32[2048,256]{0,1:T(8,128)S(1)}, u32[]{:S(2)}, u32[]{:S(2)}) %collective-permute-start) | collective-permute-done | bytes 2097184 | tf_op jit(solution)/shard_map/ppermute | solution.py:12
  191.8 1.3 copy-done.3
  193.1 3.3 collective-permute-done.1
  196.4 3.4 multiply_reduce_fusion.1
  199.8 1.3 copy-done.1
  201.1 2.6 fusion.64
  203.7 16.1 %all-reduce.1 = (f32[256]{0:T(256)S(1)}, f32[256]{0:T(256)S(1)}) all-reduce(f32[256]{0:T(256)S(1)} %get-tuple-element.74, f32[256]{0:T(256)S(1)} %get-tuple-element.62), channel_id=1, replica_groups=mesh['rows'=8,'pairs'=4] {'rows'}, use_global_device_ids=true, to_apply=%region_13.17 | all-reduce | flops 512 | bytes 4096 | tf_op jit(solution)/shard_map/psum | solution.py:63
  219.8 50.9 %all-reduce.8.cloned.1.call-done = f32[256,256]{0,1:T(8,128)} async-done(((f32[256,256]{0,1:T(8,128)}), f32[256,256]{0,1:T(8,128)}) %all-reduce.8.cloned.1.call-update) | async-done | bytes 262160 | tf_op jit(solution)/shard_map/psum | solution.py:63
  270.7 1.0 multiply_multiply_fusion
  272.6 11.7 %cholesky.164 = f32[128,128]{1,0:T(8,128)S(1)} custom-call(f32[128,128]{1,0:T(8,128)S(1)} %cholesky.197), custom_call_target="Cholesky" | custom-call | tf_op jit(solution)/shard_map/jit(cholesky)/cholesky | solution.py:16
  284.4 9.8 %custom-call.20 = f32[1,128,128]{1,2,0:T(8,128)S(1)} custom-call(f32[1,128,128]{2,1,0:T(8,128)S(1)} %get-tuple-element.89), custom_call_target="InvertDiagBlocksLowerTriangular" | custom-call | tf_op jit(solution)/shard_map/jit(cholesky)/cholesky | solution.py:16
  294.7 11.7 %cholesky.181 = f32[128,128]{1,0:T(8,128)S(1)} custom-call(f32[128,128]{1,0:T(8,128)S(1)} %convolution_subtract_fusion.4), custom_call_target="Cholesky" | custom-call | tf_op jit(solution)/shard_map/jit(cholesky)/cholesky | solution.py:16
  306.4 0.6 compare_reduce_fusion
  307.1 0.7 compare_reduce_fusion.1
  309.1 4.1 %while.9 = (s32[]{:T(128)}, f32[256,256]{1,0:T(8,128)S(1)}, s32[2,2]{1,0:T(2,128)S(1)}, f32[2,128,128]{2,1,0:T(8,128)S(1)}, s32[]{:T(128)}) while((s32[]{:T(128)}, f32[256,256]{1,0:T(8,128)S(1)}, s32[2,2]{1,0:T(2,128)S(1)}, f32[2,128,128]{2,1,0:T(8,128)S(1)}, s32[]{:T(128)}) %tuple.73), condition=%wide.while_cond.1.clone, body=%wide.while_body.1.clone.sunk | while | flops 2 | bytes 131181 | solution.py:18
  309.1 0.7 fusion.91
  309.8 1.3 bitcast_dynamic-update-slice_fusion.5
  311.1 0.7 fusion.91
  311.8 1.3 bitcast_dynamic-update-slice_fusion.5
  313.2 19.9 %custom-call.22 = f32[2,128,128]{1,2,0:T(8,128)S(1)} custom-call(f32[2,128,128]{2,1,0:T(8,128)S(1)} %get-tuple-element.39), custom_call_target="InvertDiagBlocksLowerTriangular" | custom-call | tf_op jit(solution)/shard_map/triangular_solve/custom-call.4 | solution.py:18
  336.1 0.6 fusion.21
  337.0 7.5 %fusion = f32[2048,512]{0,1:T(8,128)S(1)} fusion(f32[2048,256]{0,1:T(8,128)S(1)} %copy-done.2, f32[2048,256]{0,1:T(8,128)S(1)} %get-tuple-element.63, f32[256,256]{0,1:T(8,128)S(1)} %get-tuple-element.81, f32[256,256]{0,1:T(8,128)S(1)} %get-tuple-element.80, f32[256,256]{0,1:T(8,128)S(1)} %get-tuple-element.79, f32[256,256]{0,1:T(8,128)S(1)} %get-tuple-element.78), kind=kOutput, calls=%fused_computation.4 | convolution fusion | flops 6444285952 | bytes 9437184 | tf_op jit(solution)/shard_map/dot_general | solution.py:67
  345.1 5.5 %collective-permute-start.2 = (f32[2048,256]{0,1:T(8,128)S(1)}, f32[2048,256]{0,1:T(8,128)S(1)}, u32[]{:S(2)}, u32[]{:S(2)}) collective-permute-start(f32[2048,256]{0,1:T(8,128)S(1)} %get-tuple-element.72), channel_id=1, source_target_pairs={{0,1},{1,2},{2,3},{4,5},{5,6},{6,7},{8,9},{9,10},{10,11},{12,13},{... | collective-permute-start | bytes 6291464 | tf_op jit(solution)/shard_map/ppermute | solution.py:12
  350.6 1.9 collective-permute-start.3
  352.5 21.0 %collective-permute-done.2 = f32[2048,256]{0,1:T(8,128)S(1)} collective-permute-done((f32[2048,256]{0,1:T(8,128)S(1)}, f32[2048,256]{0,1:T(8,128)S(1)}, u32[]{:S(2)}, u32[]{:S(2)}) %collective-permute-start.2) | collective-permute-done | bytes 2097184 | tf_op jit(solution)/shard_map/ppermute | solution.py:12
  373.6 4.4 %collective-permute-done.3 = f32[2048,256]{0,1:T(8,128)S(1)} collective-permute-done((f32[2048,256]{0,1:T(8,128)S(1)}, f32[2048,256]{0,1:T(8,128)S(1)}, u32[]{:S(2)}, u32[]{:S(2)}) %collective-permute-start.3) | collective-permute-done | bytes 2097184 | tf_op jit(solution)/shard_map/ppermute | solution.py:12
  378.0 0.8 slice_select_fusion.1
  378.8 2.4 pad_maximum_fusion
  381.2 5.3 %copy.16 = f32[2048,512]{1,0:T(8,128)} copy(f32[2048,512]{0,1:T(8,128)} %pad_maximum_fusion) | data formatting | bytes 8388608 | tf_op jit(solution)/shard_map/concatenate | solution.py:76
  (63 shorter events, 11.6 us)
Async XLA Ops:
  6.5 78.0 %all-reduce.6.cloned.1.call-start = ((), (), s32[]{:S(2)}) async-start(), calls=%async_computation | async-start | bytes 524288 | tf_op jit(solution)/shard_map/psum | solution.py:63
  12.9 257.8 %all-reduce.8.cloned.1.call-start = ((), (), s32[]{:S(2)}) async-start(), calls=%async_computation.1 | async-start | bytes 524288 | tf_op jit(solution)/shard_map/psum | solution.py:63
  159.7 3.3 copy-start
  163.0 28.8 %collective-permute-start = (f32[2048,256]{0,1:T(8,128)}, f32[2048,256]{0,1:T(8,128)S(1)}, u32[]{:S(2)}, u32[]{:S(2)}) collective-permute-start(f32[2048,256]{0,1:T(8,128)} %get-tuple-element.76), channel_id=1, source_target_pairs={{0,1},{1,2},{2,3},{4,5},{5,6},{6,7},{8,9},{9,10},{10,11},{12,13},{... | collective-permute-start | bytes 6291464 | tf_op jit(solution)/shard_map/ppermute | solution.py:12
  168.5 27.9 %collective-permute-start.1 = (f32[2048,256]{0,1:T(8,128)}, f32[2048,256]{0,1:T(8,128)}, u32[]{:S(2)}, u32[]{:S(2)}) collective-permute-start(f32[2048,256]{0,1:T(8,128)} %get-tuple-element.77), channel_id=1, source_target_pairs={{1,0},{2,1},{3,2},{5,4},{6,5},{7,6},{9,8},{10,9},{11,10},{13,12},{... | collective-permute-start | bytes 6291464 | tf_op jit(solution)/shard_map/ppermute | solution.py:12
  191.8 1.3 copy-start.3
  199.8 1.3 copy-start.1
  335.4 1.6 copy-start.2
  345.1 28.5 %collective-permute-start.2 = (f32[2048,256]{0,1:T(8,128)S(1)}, f32[2048,256]{0,1:T(8,128)S(1)}, u32[]{:S(2)}, u32[]{:S(2)}) collective-permute-start(f32[2048,256]{0,1:T(8,128)S(1)} %get-tuple-element.72), channel_id=1, source_target_pairs={{0,1},{1,2},{2,3},{4,5},{5,6},{6,7},{8,9},{9,10},{10,11},{12,13},{... | collective-permute-start | bytes 6291464 | tf_op jit(solution)/shard_map/ppermute | solution.py:12
  350.6 27.4 %collective-permute-start.3 = (f32[2048,256]{0,1:T(8,128)S(1)}, f32[2048,256]{0,1:T(8,128)S(1)}, u32[]{:S(2)}, u32[]{:S(2)}) collective-permute-start(f32[2048,256]{0,1:T(8,128)S(1)} %get-tuple-element.73), channel_id=1, source_target_pairs={{1,0},{2,1},{3,2},{5,4},{6,5},{7,6},{9,8},{10,9},{11,10},{13,12},{... | collective-permute-start | bytes 6291464 | tf_op jit(solution)/shard_map/ppermute | solution.py:12
Sparse Core Ops, SparseCore 0:
  13.1 71.4 all-reduce.5
  203.8 66.8 all-reduce.7
where the time goes:
time: 398 us; the launch traced here: 394 us
  waiting for transfers between devices  151 us (38%)
  other arithmetic  124 us (31%)
  blocking collectives  35.1 us (9%)
  matrix products  34.3 us (9%)
  local copies, waits for them, and re-layouts  17.8 us (4%)
  between operations  16.7 us (4%)
  starting transfers between devices  14.9 us (4%)
    psum x2, waiting for transfers between devices, shards(): lax.psum((cross_local, first_local, second_local), 'rows')  101 us
    another operation x14, other arithmetic, spd_solve(): factor = jnp.linalg.cholesky(system)  69.3 us
    ppermute x4, waiting for transfers between devices, passed_along(): return lax.ppermute(value, axis, pairs)  50 us
    another operation x5, other arithmetic, spd_solve(): lax.linalg.triangular_solve(factor, middle, left_side=True, lower=True, t...  40 us
    psum x2, blocking collectives, shards(): lax.psum((cross_local, first_local, second_local), 'rows')  35.1 us
    dot_general x2, matrix products, shards(): jnp.dot(both, rotate, precision=precise, preferred_element_type=jnp.float32)  16.3 us
    ppermute x4, starting transfers between devices, passed_along(): return lax.ppermute(value, axis, pairs)  14.8 us
    dot_general x2, matrix products, shards(): lax.dot_general(first_block, second_block, (((0,), (0,)), ((), ())), prec...  8.95 us
  transfers between devices with their start and end apart: 6, of which 6 were waited for; matrix products, arithmetic and copies ran while one was open for 1% of the time, Pallas kernels for 0%

commit v1 on v0

v1 whole, which is shorter than its diff:
```python
import functools

import jax
import jax.numpy as jnp
from jax import lax
from jax.experimental import pallas as pl
from jax.experimental.pallas import tpu as pltpu
from jax.sharding import PartitionSpec as P

STEPS = 2
CHUNKS = 8
F32 = jnp.float32
BF16 = jnp.bfloat16
MESH = pl.DeviceIdType.MESH


def split(value):
    high = value.astype(BF16)
    return high, (value - high.astype(F32)).astype(BF16)


def dot_bf16(left, right, left_dim):
    return lax.dot_general(
        left, right, (((left_dim,), (0,)), ((), ())), preferred_element_type=F32
    )


def dot_three(left, right, left_dim):
    return (
        dot_bf16(left[0], right[1], left_dim)
        + dot_bf16(left[1], right[0], left_dim)
        + dot_bf16(left[0], right[0], left_dim)
    )


def exact_dot(left, right, left_dim=1):
    return lax.dot_general(
        left,
        right,
        (((left_dim,), (0,)), ((), ())),
        precision=lax.Precision.HIGHEST,
        preferred_element_type=F32,
    )


def sum_over_rows(count, part, total, recv, mine, gathered, sems):
    send_one, recv_one, send_two, recv_two = sems
    me = lax.axis_index("rows")
    first_copies = []
    for far in range(1, count):
        peer = lax.rem(me + far, count)
        copy = pltpu.make_async_remote_copy(
            src_ref=part.at[peer],
            dst_ref=recv.at[far],
            send_sem=send_one.at[far],
            recv_sem=recv_one.at[far],
            device_id={"rows": peer},
            device_id_type=MESH,
        )
        copy.start()
        first_copies.append(copy)
    acc = part[me]
    for far in range(1, count):
        first_copies[far - 1].wait_recv()
        acc = acc + recv[far]
    mine[...] = acc
    second_copies = []
    for far in range(1, count):
        peer = lax.rem(me + far, count)
        copy = pltpu.make_async_remote_copy(
            src_ref=mine,
            dst_ref=gathered.at[far],
            send_sem=send_two.at[far],
            recv_sem=recv_two.at[far],
            device_id={"rows": peer},
            device_id_type=MESH,
        )
        copy.start()
        second_copies.append(copy)
    total[me] = acc
    for far in range(1, count):
        second_copies[far - 1].wait_recv()
        total[lax.rem(me + count - far, count)] = gathered[far]
    for copy in first_copies + second_copies:
        copy.wait_send()


def stage_kernel(rotates, sums, count, length, *refs):
    refs = list(refs)
    matrix = refs.pop(0)
    if rotates:
        rot_high, rot_low = refs.pop(0), refs.pop(0)
        moved = refs.pop(0)
    if sums:
        total = refs.pop(0)
    loaded, load_sem = refs.pop(0), refs.pop(0)
    if rotates:
        up, other, land_first, land_second = (refs.pop(0) for _ in range(4))
        up_send, up_recv, down_send, down_recv, store_sem = (refs.pop(0) for _ in range(5))
    if sums:
        cross, norms, part, recv, mine, gathered = (refs.pop(0) for _ in range(6))
        sums_sems = tuple(refs.pop(0) for _ in range(4))
    rows, cols = loaded.shape
    block = cols // 2
    step = rows // CHUNKS
    position = lax.axis_index("pairs")
    lowest = position == 0
    highest = position == length - 1

    def at(chunk):
        return pl.ds(pl.multiple_of(chunk * step, step), step)

    def load(chunk):
        return pltpu.make_async_copy(
            matrix.at[at(chunk)], loaded.at[at(chunk)], load_sem.at[chunk]
        )

    def to_upper(chunk):
        return pltpu.make_async_remote_copy(
            src_ref=up.at[at(chunk)],
            dst_ref=land_first.at[at(chunk)],
            send_sem=up_send.at[chunk],
            recv_sem=up_recv.at[chunk],
            device_id={"pairs": lax.rem(position + 1, length)},
            device_id_type=MESH,
        )

    def to_lower(chunk):
        return pltpu.make_async_remote_copy(
            src_ref=other.at[at(chunk)],
            dst_ref=land_second.at[at(chunk)],
            send_sem=down_send.at[chunk],
            recv_sem=down_recv.at[chunk],
            device_id={"pairs": lax.rem(position + length - 1, length)},
            device_id_type=MESH,
        )

    def store(chunk, half):
        source = land_second if half else land_first
        return pltpu.make_async_copy(
            source.at[at(chunk)],
            moved.at[at(chunk), pl.ds(half * block, block)],
            store_sem.at[half, chunk],
        )

    for chunk in range(CHUNKS):
        load(chunk).start()

    barrier = pltpu.get_barrier_semaphore()
    if sums:
        me = lax.axis_index("rows")
        for far in range(1, count):
            pl.semaphore_signal(
                barrier,
                inc=1,
                device_id={"rows": lax.rem(me + far, count)},
                device_id_type=MESH,
            )
    greeted = jnp.int32(count - 1 if sums else 0)
    if rotates:
        @pl.when(jnp.logical_not(lowest))
        def _():
            pl.semaphore_signal(
                barrier, inc=1, device_id={"pairs": position - 1}, device_id_type=MESH
            )

        @pl.when(jnp.logical_not(highest))
        def _():
            pl.semaphore_signal(
                barrier, inc=1, device_id={"pairs": position + 1}, device_id_type=MESH
            )

        greeted = greeted + jnp.where(lowest, 0, 1) + jnp.where(highest, 0, 1)
    pl.semaphore_wait(barrier, greeted)

    if rotates:
        def turn(chunk, carry):
            load(chunk).wait()
            turned = dot_three(split(loaded[at(chunk), :]), (rot_high[...], rot_low[...]), 1)
            left, right = turned[:, :block], turned[:, block:]
            up[at(chunk), :] = jnp.where(lowest, right, left)
            other[at(chunk), :] = jnp.where(lowest, left, right)

            @pl.when(jnp.logical_not(highest))
            def _():
                to_upper(chunk).start()

            @pl.when(highest)
            def _():
                land_second[at(chunk), :] = left

            @pl.when(jnp.logical_not(lowest))
            def _():
                to_lower(chunk).start()

            @pl.when(lowest)
            def _():
                land_first[at(chunk), :] = left

            return carry

        lax.fori_loop(0, CHUNKS, turn, 0)

    if sums:
        cross[...] = jnp.zeros_like(cross)
        norms[...] = jnp.zeros_like(norms)

    def take(chunk, carry):
        if rotates:
            @pl.when(jnp.logical_not(lowest))
            def _():
                to_upper(chunk).wait_recv()

            @pl.when(jnp.logical_not(highest))
            def _():
                to_lower(chunk).wait_recv()

            store(chunk, 0).start()
            store(chunk, 1).start()
        else:
            load(chunk).wait()
        if sums:
            if rotates:
                first, second = land_first[at(chunk), :], land_second[at(chunk), :]
            else:
                first, second = loaded[at(chunk), :block], loaded[at(chunk), block:]
            cross[...] += dot_three(split(first), split(second), 0)
            norms[0:1, :] += jnp.sum(first * first, axis=0, keepdims=True)
            norms[1:2, :] += jnp.sum(second * second, axis=0, keepdims=True)
        return carry

    lax.fori_loop(0, CHUNKS, take, 0)

    if sums:
        share = block // count
        half = block // 2
        for slot in range(count):
            part[slot, :share, :] = cross[slot * share : (slot + 1) * share, :half]
            part[slot, share : 2 * share, :] = cross[slot * share : (slot + 1) * share, half:]
            part[slot, 2 * share : 2 * share + 8, :] = norms[:, :half]
            part[slot, 2 * share + 8 : 2 * share + 16, :] = norms[:, half:]
        sum_over_rows(count, part, total, recv, mine, gathered, sums_sems)

    if rotates:
        def finish(chunk, carry):
            @pl.when(jnp.logical_not(highest))
            def _():
                to_upper(chunk).wait_send()

            @pl.when(jnp.logical_not(lowest))
            def _():
                to_lower(chunk).wait_send()

            store(chunk, 0).wait()
            store(chunk, 1).wait()
            return carry

        lax.fori_loop(0, CHUNKS, finish, 0)


def stage(name, number, matrix, rotation, sums):
    rows, cols = matrix.shape
    block = cols // 2
    count = lax.axis_size("rows")
    length = lax.axis_size("pairs")
    rotates = rotation is not None
    slot = (2 * (block // count) + 16, block // 2)
    hbm = pl.BlockSpec(memory_space=pl.ANY)
    vmem = pl.BlockSpec(memory_space=pltpu.VMEM)
    dma = pltpu.SemaphoreType.DMA
    in_specs, outs, out_specs = [hbm], [], []
    scratch = [pltpu.VMEM((rows, cols), F32), dma((CHUNKS,))]
    if rotates:
        in_specs += [vmem, vmem]
        outs.append(jax.ShapeDtypeStruct((rows, cols), F32))
        out_specs.append(hbm)
        scratch += [pltpu.VMEM((rows, block), F32)] * 4
        scratch += [dma((CHUNKS,))] * 4 + [dma((2, CHUNKS))]
    if sums:
        outs.append(jax.ShapeDtypeStruct((count,) + slot, F32))
        out_specs.append(vmem)
        scratch += [pltpu.VMEM((block, block), F32), pltpu.VMEM((8, block), F32)]
        scratch += [pltpu.VMEM((count,) + slot, F32)] * 2 + [pltpu.VMEM(slot, F32)]
        scratch += [pltpu.VMEM((count,) + slot, F32)]
        scratch += [dma((count,))] * 4
    return pl.pallas_call(
        functools.partial(stage_kernel, rotates, sums, count, length),
        out_shape=outs,
        in_specs=in_specs,
        out_specs=out_specs,
        scratch_shapes=scratch,
        name=name,
        compiler_params=pltpu.CompilerParams(
            collective_id=number, has_side_effects=True, vmem_limit_bytes=50 * 2**20
        ),
    )(matrix, *(rotation or ()))


def rotation_kernel(rows_all, total, rot_high, rot_low, coupling, inverse, residual):
    count, depth, half = total.shape
    block = 2 * half
    share = (depth - 16) // 2
    for slot in range(count):
        coupling[slot * share : (slot + 1) * share, :half] = total[slot, :share, :]
        coupling[slot * share : (slot + 1) * share, half:] = total[slot, share : 2 * share, :]
    norms = jnp.concatenate(
        [total[0, 2 * share : 2 * share + 8, :], total[0, 2 * share + 8 :, :]], axis=1
    )
    scales = lax.rsqrt(norms / rows_all + 1e-06)
    row = lax.broadcasted_iota(jnp.int32, (block, block), 0)
    col = lax.broadcasted_iota(jnp.int32, (block, block), 1)
    identity = jnp.where(row == col, 1.0, 0.0).astype(F32)
    scale_first = jnp.sum(identity * scales[0:1, :], axis=1, keepdims=True)
    coupling[...] = 0.5 * coupling[...] * scale_first * scales[1:2, :] / rows_all
    turn = coupling[...]
    gram = lax.dot_general(
        turn,
        turn,
        (((1,), (1,)), ((), ())),
        precision=lax.Precision.HIGHEST,
        preferred_element_type=F32,
    )
    spread = jnp.max(jnp.sum(jnp.abs(gram), axis=1, keepdims=True))
    start = 2.0 / (2.0 + spread)
    first = (1.0 - start) * identity - start * gram
    inverse[...] = start * (identity + first)
    bound = spread / (2.0 + spread)
    residual[...] = exact_dot(first, first)

    def grow(state):
        limit, trips = state
        both = exact_dot(jnp.concatenate([inverse[...], residual[...]], axis=0), residual[...])
        inverse[...] += both[:block]
        residual[...] = both[block:]
        return limit * limit, trips + 1

    lax.while_loop(
        lambda state: jnp.logical_and(state[0] > 1e-07, state[1] < 30),
        grow,
        (bound * bound, jnp.int32(0)),
    )

    def correct(index, carry):
        guess = inverse[...]
        residual[...] = identity - guess - exact_dot(gram, guess)
        inverse[...] = guess + exact_dot(guess, residual[...])
        return carry

    lax.fori_loop(0, jnp.where(spread > 32.0, 4, 0), correct, 0)
    upper = exact_dot(inverse[...], turn)
    lower = exact_dot(turn, upper, 0)
    parts = (
        (0, 0, 2.0 * inverse[...] - identity),
        (0, 1, 2.0 * upper),
        (1, 0, -2.0 * upper.T),
        (1, 1, identity - 2.0 * lower),
    )
    for down, across, value in parts:
        high, low = split(value)
        where = (pl.ds(down * block, block), pl.ds(across * block, block))
        rot_high[where] = high
        rot_low[where] = low


def rotation_of(total, rows_all):
    block = 2 * total.shape[2]
    vmem = pl.BlockSpec(memory_space=pltpu.VMEM)
    return pl.pallas_call(
        functools.partial(rotation_kernel, rows_all),
        out_shape=[jax.ShapeDtypeStruct((2 * block, 2 * block), BF16)] * 2,
        in_specs=[vmem],
        out_specs=[vmem, vmem],
        scratch_shapes=[pltpu.VMEM((block, block), F32)] * 3,
        name="rotation",
        compiler_params=pltpu.CompilerParams(vmem_limit_bytes=32 * 2**20),
    )(total)


def shards(matrix):
    rows_all = matrix.shape[0] * lax.axis_size("rows")
    (total,) = stage("products", 0, matrix, None, True)
    for turn_index in range(STEPS - 1):
        rotation = rotation_of(total, rows_all)
        matrix, total = stage("turn_and_products", 1, matrix, rotation, True)
    rotation = rotation_of(total, rows_all)
    (matrix,) = stage("last_turn", 2, matrix, rotation, False)
    return matrix


def solution(mesh):
    return jax.shard_map(
        shards,
        mesh=mesh,
        in_specs=(P("rows", "pairs"),),
        out_specs=P("rows", "pairs"),
        check_vma=False,
    )
```

time: 398 us -> 109 us (0.27); the launches traced: 394 us -> 109 us
  waiting for transfers between devices: 151 us -> 0 us
  other arithmetic: 124 us -> 0 us
  Pallas kernels: 0 us -> 104 us
  blocking collectives: 35.1 us -> 0 us
  matrix products: 34.3 us -> 0 us
  between operations: 16.7 us -> 0.04 us
  starting transfers between devices: 14.9 us -> 0 us
  local copies, waits for them, and re-layouts: 17.8 us -> 4.64 us
    another operation x19 -> x0, other arithmetic: 109 us -> none  [the longest x14 69.3 us: spd_solve(): factor = jnp.linalg.cholesky(system)]
    pallas_call x0 -> x5, Pallas kernels: none -> 104 us  [the longest x3 92.3 us: stage(): pl.pallas_call(functools.partial(stage_kernel, rotates, sums, count, leng...]
    psum x2 -> x0, waiting for transfers between devices: 101 us -> none  [shards(): lax.psum((cross_local, first_local, second_local), 'rows')]
    ppermute x4 -> x0, waiting for transfers between devices: 50 us -> none  [passed_along(): return lax.ppermute(value, axis, pairs)]
    psum x2 -> x0, blocking collectives: 35.1 us -> none  [shards(): lax.psum((cross_local, first_local, second_local), 'rows')]
    dot_general x8 -> x0, matrix products: 27.7 us -> none  [the longest x2 16.3 us: shards(): jnp.dot(both, rotate, precision=precise, preferred_element_type=jnp.float32)]
    ppermute x4 -> x0, starting transfers between devices: 14.8 us -> none  [passed_along(): return lax.ppermute(value, axis, pairs)]
    another operation x21 -> x0, local copies, waits for them, and re-layouts: 8.46 us -> none  [the longest x17 8.41 us: spd_solve(): lax.linalg.triangular_solve(factor, middle, left_side=True, lower=True, t...]
  transfers between devices with their start and end apart: 6 -> 0, of which waited for: 6 -> 0; matrix products, arithmetic and copies ran while one was open for 1% -> 0% of each run, Pallas kernels for 0% -> 0%
where the time goes in v1:
time: 109 us
  Pallas kernels  104 us (95%)
  local copies, waits for them, and re-layouts  4.64 us (4%)
    pallas_call x3, Pallas kernels, stage(): pl.pallas_call(functools.partial(stage_kernel, rotates, sums, count, leng...  92.3 us
    pallas_call x2, Pallas kernels, rotation_of(): pl.pallas_call(functools.partial(rotation_kernel, rows_all), out_shape=[j...  11.6 us
    unnamed x1, local copies, waits for them, and re-layouts  4.64 us

profile of v1, /device:TPU:1, one launch (start us, length us, event | category | flops | bytes accessed | tf_op | source)
XLA Modules:
  0.0 108.6 jit_solution(3396030664486308395)
XLA Ops:
  0.0 20.1 %products.1.total = f32[8,80,128]{2,1,0:T(8,128)S(1)} custom-call(f32[2048,512]{1,0:T(8,128)} %refs_0_.3), custom_call_target="tpu_custom_call" | custom-call | tf_op jit(solution)/shard_map/products/pallas_call | solution.py:286
  20.1 5.5 %rotation.2 = (bf16[512,512]{1,0:T(8,128)(2,1)S(1)}, bf16[512,512]{1,0:T(8,128)(2,1)S(1)}) custom-call(f32[8,80,128]{2,1,0:T(8,128)S(1)} %products.1.total), custom_call_target="tpu_custom_call" | custom-call | tf_op jit(solution)/shard_map/rotation/pallas_call | solution.py:368
  25.6 44.6 %turn_and_products.1 = (f32[2048,512]{1,0:T(8,128)}, f32[8,80,128]{2,1,0:T(8,128)S(1)}) custom-call(f32[2048,512]{1,0:T(8,128)} %refs_0_.3, bf16[512,512]{1,0:T(8,128)(2,1)S(1)} %get-tuple-element.11.refs_1_, bf16[512,512]{1,0:T(8,128)(2,1)S(1)} %get-tuple-element.12.refs_2_), custom_call_target="tpu_custom_call" | custom-call | tf_op jit(solution)/shard_map/turn_and_products/pallas_call | solution.py:286
  70.2 6.1 %rotation.3 = (bf16[512,512]{1,0:T(8,128)(2,1)S(1)}, bf16[512,512]{1,0:T(8,128)(2,1)S(1)}) custom-call(f32[8,80,128]{2,1,0:T(8,128)S(1)} %get-tuple-element.14.total), custom_call_target="tpu_custom_call" | custom-call | tf_op jit(solution)/shard_map/rotation/pallas_call | solution.py:368
  76.4 27.6 %last_turn.1 = f32[2048,512]{1,0:T(8,128)} custom-call(f32[2048,512]{1,0:T(8,128)} %get-tuple-element.13.refs_0_, bf16[512,512]{1,0:T(8,128)(2,1)S(1)} %get-tuple-element.15.refs_1_, bf16[512,512]{1,0:T(8,128)(2,1)S(1)} %get-tuple-element.16.refs_2_), custom_call_target="tpu_custom_call" | custom-call | tf_op jit(solution)/shard_map/last_turn/pallas_call | solution.py:286
  104.0 4.6 %copy.3 = f32[2048,512]{1,0:T(8,128)} copy(f32[2048,512]{1,0:T(8,128)} %last_turn.1) | data formatting | bytes 8388608

commit v2 on v1

--- a/solution.py
+++ b/solution.py
@@ -7,8 +7,8 @@
 from jax.experimental.pallas import tpu as pltpu
 from jax.sharding import PartitionSpec as P
 
-STEPS = 2
 CHUNKS = 8
+LATE = 2
 F32 = jnp.float32
 BF16 = jnp.bfloat16
 MESH = pl.DeviceIdType.MESH
@@ -43,7 +43,7 @@
     )
 
 
-def sum_over_rows(count, part, total, recv, mine, gathered, sems):
+def sum_over_rows(count, part, total, recv, mine, gathered, sems, beside):
     send_one, recv_one, send_two, recv_two = sems
     me = lax.axis_index("rows")
     first_copies = []
@@ -77,22 +77,57 @@
         )
         copy.start()
         second_copies.append(copy)
+    if beside:
+        partner, has_partner, total_near, gathered_near, send_near, recv_near = beside
+
+        def to_near(far):
+            return pltpu.make_async_remote_copy(
+                src_ref=mine,
+                dst_ref=gathered_near.at[far],
+                send_sem=send_near.at[far],
+                recv_sem=recv_near.at[far],
+                device_id={"rows": lax.rem(me + far, count), "pairs": partner},
+                device_id_type=MESH,
+            )
+
+        @pl.when(has_partner)
+        def _():
+            for far in range(count):
+                to_near(far).start()
+
     total[me] = acc
     for far in range(1, count):
         second_copies[far - 1].wait_recv()
         total[lax.rem(me + count - far, count)] = gathered[far]
+    if beside:
+        @pl.when(has_partner)
+        def _():
+            for far in range(count):
+                to_near(far).wait_recv()
+                total_near[lax.rem(me + count - far, count)] = gathered_near[far]
+            for far in range(count):
+                to_near(far).wait_send()
+
+        @pl.when(jnp.logical_not(has_partner))
+        def _():
+            total_near[...] = total[...]
+
     for copy in first_copies + second_copies:
         copy.wait_send()
 
 
-def stage_kernel(rotates, sums, count, length, *refs):
+def stage_kernel(rotates, sums, ahead, count, length, *refs):
     refs = list(refs)
     matrix = refs.pop(0)
     if rotates:
         rot_high, rot_low = refs.pop(0), refs.pop(0)
+        if ahead and not sums:
+            kept, extra, near_high, near_low = (refs.pop(0) for _ in range(4))
         moved = refs.pop(0)
     if sums:
         total = refs.pop(0)
+        if ahead:
+            kept, extra, total_near = (refs.pop(0) for _ in range(3))
     loaded, load_sem = refs.pop(0), refs.pop(0)
     if rotates:
         up, other, land_first, land_second = (refs.pop(0) for _ in range(4))
@@ -100,12 +135,29 @@
     if sums:
         cross, norms, part, recv, mine, gathered = (refs.pop(0) for _ in range(6))
         sums_sems = tuple(refs.pop(0) for _ in range(4))
+    if ahead and sums:
+        land_extra, gathered_near = refs.pop(0), refs.pop(0)
+        extra_send, extra_recv, send_near, recv_near, side_sem = (refs.pop(0) for _ in range(5))
+    if ahead and not sums:
+        had_kept, had_extra, side_sem = (refs.pop(0) for _ in range(3))
     rows, cols = loaded.shape
     block = cols // 2
     step = rows // CHUNKS
     position = lax.axis_index("pairs")
     lowest = position == 0
     highest = position == length - 1
+    odd = lax.rem(position, 2) == 1
+    even = jnp.logical_not(odd)
+    has_partner = jnp.logical_or(
+        jnp.logical_and(odd, position < length - 1), jnp.logical_and(even, position > 0)
+    )
+    sends_extra = jnp.logical_or(
+        jnp.logical_and(even, position + 2 < length), jnp.logical_and(odd, position >= 2)
+    )
+    gets_extra = jnp.logical_or(
+        jnp.logical_and(even, position >= 2), jnp.logical_and(odd, position + 2 < length)
+    )
+    partner = lax.rem(position + jnp.where(odd, 1, length - 1), length)
 
     def at(chunk):
         return pl.ds(pl.multiple_of(chunk * step, step), step)
@@ -143,8 +195,35 @@
             store_sem.at[half, chunk],
         )
 
+    def to_extra(chunk, source, target):
+        return pltpu.make_async_remote_copy(
+            src_ref=source.at[at(chunk)],
+            dst_ref=land_extra.at[at(chunk)],
+            send_sem=extra_send.at[chunk],
+            recv_sem=extra_recv.at[chunk],
+            device_id={"pairs": lax.rem(target + length, length)},
+            device_id_type=MESH,
+        )
+
+    def keep(chunk, source):
+        return pltpu.make_async_copy(source.at[at(chunk)], kept.at[at(chunk)], side_sem.at[0, chunk])
+
+    def store_extra(chunk):
+        return pltpu.make_async_copy(
+            land_extra.at[at(chunk)], extra.at[at(chunk)], side_sem.at[1, chunk]
+        )
+
+    def load_side(chunk):
+        return (
+            pltpu.make_async_copy(kept.at[at(chunk)], had_kept.at[at(chunk)], side_sem.at[0, chunk]),
+            pltpu.make_async_copy(extra.at[at(chunk)], had_extra.at[at(chunk)], side_sem.at[1, chunk]),
+        )
+
     for chunk in range(CHUNKS):
         load(chunk).start()
+        if ahead and not sums and chunk >= LATE:
+            for copy in load_side(chunk):
+                copy.start()
 
     barrier = pltpu.get_barrier_semaphore()
     if sums:
@@ -171,6 +250,31 @@
             )
 
         greeted = greeted + jnp.where(lowest, 0, 1) + jnp.where(highest, 0, 1)
+    if ahead and sums:
+        @pl.when(position >= 2)
+        def _():
+            pl.semaphore_signal(
+                barrier, inc=1, device_id={"pairs": position - 2}, device_id_type=MESH
+            )
+
+        @pl.when(position + 2 < length)
+        def _():
+            pl.semaphore_signal(
+                barrier, inc=1, device_id={"pairs": position + 2}, device_id_type=MESH
+            )
+
+        @pl.when(has_partner)
+        def _():
+            for far in range(1, count):
+                pl.semaphore_signal(
+                    barrier,
+                    inc=1,
+                    device_id={"rows": lax.rem(me + far, count), "pairs": partner},
+                    device_id_type=MESH,
+                )
+
+        greeted = greeted + jnp.where(position >= 2, 1, 0) + jnp.where(position + 2 < length, 1, 0)
+        greeted = greeted + jnp.where(has_partner, count - 1, 0)
     pl.semaphore_wait(barrier, greeted)
 
     if rotates:
@@ -199,19 +303,94 @@
 
             return carry
 
-        lax.fori_loop(0, CHUNKS, turn, 0)
+        if ahead and not sums:
+            lax.fori_loop(0, LATE, turn, 0)
+
+            @pl.when(jnp.logical_not(has_partner))
+            def _():
+                lax.fori_loop(LATE, CHUNKS, turn, 0)
+
+            @pl.when(has_partner)
+            def _():
+                inner = pl.ds(pl.multiple_of(jnp.where(odd, block, 0), block), block)
+
+                def turn_near(chunk, carry):
+                    load(chunk).wait()
+                    sent = dot_three(
+                        split(loaded[at(chunk), :]), (rot_high[:, inner], rot_low[:, inner]), 1
+                    )
+
+                    @pl.when(odd)
+                    def _():
+                        other[at(chunk), :] = sent
+                        to_lower(chunk).start()
+
+                    @pl.when(even)
+                    def _():
+                        up[at(chunk), :] = sent
+                        to_upper(chunk).start()
+
+                    mine_block, far_block = had_kept[at(chunk), :], had_extra[at(chunk), :]
+                    pair = jnp.concatenate(
+                        [
+                            jnp.where(odd, mine_block, far_block),
+                            jnp.where(odd, far_block, mine_block),
+                        ],
+                        axis=1,
+                    )
+                    stays = dot_three(split(pair), (near_high[...], near_low[...]), 1)
+
+                    @pl.when(odd)
+                    def _():
+                        land_second[at(chunk), :] = stays
+
+                    @pl.when(even)
+                    def _():
+                        land_first[at(chunk), :] = stays
+
+                    return carry
+
+                for chunk in range(LATE, CHUNKS):
+                    for copy in load_side(chunk):
+                        copy.wait()
+                lax.fori_loop(LATE, CHUNKS, turn_near, 0)
+
+            @pl.when(jnp.logical_not(has_partner))
+            def _():
+                for chunk in range(LATE, CHUNKS):
+                    for copy in load_side(chunk):
+                        copy.wait()
+        else:
+            lax.fori_loop(0, CHUNKS, turn, 0)
+
+        if ahead and sums:
+            for chunk in range(LATE, CHUNKS):
+                @pl.when(odd)
+                def _():
+                    keep(chunk, up).start()
+
+                @pl.when(even)
+                def _():
+                    keep(chunk, other).start()
 
     if sums:
         cross[...] = jnp.zeros_like(cross)
         norms[...] = jnp.zeros_like(norms)
 
+    def gets(chunk, edge, far_side):
+        arrives = jnp.logical_not(edge)
+        if ahead and not sums:
+            own = jnp.logical_and(far_side, chunk >= LATE)
+            arrives = jnp.logical_and(arrives, jnp.logical_not(own))
+        return arrives
+
     def take(chunk, carry):
         if rotates:
-            @pl.when(jnp.logical_not(lowest))
+            @pl.when(gets(chunk, lowest, even))
             def _():
                 to_upper(chunk).wait_recv()
 
-            @pl.when(jnp.logical_not(highest))
+            @pl.when(gets(chunk, highest, odd))
             def _():
                 to_lower(chunk).wait_recv()
 
@@ -239,15 +418,42 @@
             part[slot, share : 2 * share, :] = cross[slot * share : (slot + 1) * share, half:]
             part[slot, 2 * share : 2 * share + 8, :] = norms[:, :half]
             part[slot, 2 * share + 8 : 2 * share + 16, :] = norms[:, half:]
-        sum_over_rows(count, part, total, recv, mine, gathered, sums_sems)
+        beside = None
+        if ahead:
+            beside = (partner, has_partner, total_near, gathered_near, send_near, recv_near)
+        sum_over_rows(count, part, total, recv, mine, gathered, sums_sems, beside)
+    if ahead and sums:
+        @pl.when(jnp.logical_and(sends_extra, even))
+        def _():
+            for chunk in range(LATE, CHUNKS):
+                to_extra(chunk, up, position + 2).start()
+
+        @pl.when(jnp.logical_and(sends_extra, odd))
+        def _():
+            for chunk in range(LATE, CHUNKS):
+                to_extra(chunk, other, position - 2).start()
+
+        for chunk in range(LATE, CHUNKS):
+            @pl.when(gets_extra)
+            def _():
+                to_extra(chunk, up, position).wait_recv()
+
+            store_extra(chunk).start()
+        for chunk in range(LATE, CHUNKS):
+            @pl.when(sends_extra)
+            def _():
+                to_extra(chunk, up, position).wait_send()
+
+            keep(chunk, up).wait()
+            store_extra(chunk).wait()
 
     if rotates:
         def finish(chunk, carry):
-            @pl.when(jnp.logical_not(highest))
+            @pl.when(gets(chunk, highest, odd))
             def _():
                 to_upper(chunk).wait_send()
 
-            @pl.when(jnp.logical_not(lowest))
+            @pl.when(gets(chunk, lowest, even))
             def _():
                 to_lower(chunk).wait_send()
 
@@ -258,7 +464,7 @@
         lax.fori_loop(0, CHUNKS, finish, 0)
 
 
-def stage(name, number, matrix, rotation, sums):
+def stage(name, number, matrix, rotation, sums, ahead=False, side=()):
     rows, cols = matrix.shape
     block = cols // 2
     count = lax.axis_size("rows")
@@ -272,6 +478,8 @@
     scratch = [pltpu.VMEM((rows, cols), F32), dma((CHUNKS,))]
     if rotates:
         in_specs += [vmem, vmem]
+        if side:
+            in_specs += [hbm, hbm, vmem, vmem]
         outs.append(jax.ShapeDtypeStruct((rows, cols), F32))
         out_specs.append(hbm)
         scratch += [pltpu.VMEM((rows, block), F32)] * 4
@@ -279,12 +487,20 @@
     if sums:
         outs.append(jax.ShapeDtypeStruct((count,) + slot, F32))
         out_specs.append(vmem)
+        if ahead:
+            outs += [jax.ShapeDtypeStruct((rows, block), F32)] * 2 + [outs[-1]]
+            out_specs += [hbm, hbm, vmem]
         scratch += [pltpu.VMEM((block, block), F32), pltpu.VMEM((8, block), F32)]
         scratch += [pltpu.VMEM((count,) + slot, F32)] * 2 + [pltpu.VMEM(slot, F32)]
         scratch += [pltpu.VMEM((count,) + slot, F32)]
         scratch += [dma((count,))] * 4
+    if ahead and sums:
+        scratch += [pltpu.VMEM((rows, block), F32), pltpu.VMEM((count,) + slot, F32)]
+        scratch += [dma((CHUNKS,))] * 2 + [dma((count,))] * 2 + [dma((2, CHUNKS))]
+    if ahead and not sums:
+        scratch += [pltpu.VMEM((rows, block), F32)] * 2 + [dma((2, CHUNKS))]
     return pl.pallas_call(
-        functools.partial(stage_kernel, rotates, sums, count, length),
+        functools.partial(stage_kernel, rotates, sums, ahead, count, length),
         out_shape=outs,
         in_specs=in_specs,
         out_specs=out_specs,
@@ -293,45 +509,58 @@
         compiler_params=pltpu.CompilerParams(
             collective_id=number, has_side_effects=True, vmem_limit_bytes=50 * 2**20
         ),
-    )(matrix, *(rotation or ()))
-
-
-def rotation_kernel(rows_all, total, rot_high, rot_low, coupling, inverse, residual):
-    count, depth, half = total.shape
+    )(matrix, *(rotation or ()), *side)
+
+
+def rotation_kernel(rows_all, problems, *refs):
+    totals, refs = refs[:problems], refs[problems:]
+    outs, (coupling, inverse, residual) = refs[: 2 * problems], refs[2 * problems :]
+    count, depth, half = totals[0].shape
     block = 2 * half
     share = (depth - 16) // 2
-    for slot in range(count):
-        coupling[slot * share : (slot + 1) * share, :half] = total[slot, :share, :]
-        coupling[slot * share : (slot + 1) * share, half:] = total[slot, share : 2 * share, :]
-    norms = jnp.concatenate(
-        [total[0, 2 * share : 2 * share + 8, :], total[0, 2 * share + 8 :, :]], axis=1
-    )
-    scales = lax.rsqrt(norms / rows_all + 1e-06)
     row = lax.broadcasted_iota(jnp.int32, (block, block), 0)
     col = lax.broadcasted_iota(jnp.int32, (block, block), 1)
     identity = jnp.where(row == col, 1.0, 0.0).astype(F32)
-    scale_first = jnp.sum(identity * scales[0:1, :], axis=1, keepdims=True)
-    coupling[...] = 0.5 * coupling[...] * scale_first * scales[1:2, :] / rows_all
-    turn = coupling[...]
-    gram = lax.dot_general(
-        turn,
-        turn,
-        (((1,), (1,)), ((), ())),
-        precision=lax.Precision.HIGHEST,
-        preferred_element_type=F32,
-    )
-    spread = jnp.max(jnp.sum(jnp.abs(gram), axis=1, keepdims=True))
-    start = 2.0 / (2.0 + spread)
-    first = (1.0 - start) * identity - start * gram
-    inverse[...] = start * (identity + first)
-    bound = spread / (2.0 + spread)
-    residual[...] = exact_dot(first, first)
+
+    def gram_of(turn):
+        return lax.dot_general(
+            turn,
+            turn,
+            (((1,), (1,)), ((), ())),
+            precision=lax.Precision.HIGHEST,
+            preferred_element_type=F32,
+        )
+
+    spread_most = None
+    for index, total in enumerate(totals):
+        for slot in range(count):
+            rows = slice(slot * share, (slot + 1) * share)
+            coupling[index, rows, :half] = total[slot, :share, :]
+            coupling[index, rows, half:] = total[slot, share : 2 * share, :]
+        norms = jnp.concatenate(
+            [total[0, 2 * share : 2 * share + 8, :], total[0, 2 * share + 8 :, :]], axis=1
+        )
+        scales = lax.rsqrt(norms / rows_all + 1e-06)
+        scale_first = jnp.sum(identity * scales[0:1, :], axis=1, keepdims=True)
+        turn = 0.5 * coupling[index] * scale_first * scales[1:2, :] / rows_all
+        coupling[index] = turn
+        gram = gram_of(turn)
+        spread = jnp.max(jnp.sum(jnp.abs(gram), axis=1, keepdims=True))
+        start = 2.0 / (2.0 + spread)
+        first = (1.0 - start) * identity - start * gram
+        inverse[index] = start * (identity + first)
+        residual[index] = exact_dot(first, first)
+        spread_most = spread if index == 0 else jnp.maximum(spread_most, spread)
+    bound = spread_most / (2.0 + spread_most)
 
     def grow(state):
         limit, trips = state
-        both = exact_dot(jnp.concatenate([inverse[...], residual[...]], axis=0), residual[...])
-        inverse[...] += both[:block]
-        residual[...] = both[block:]
+        for index in range(problems):
+            both = exact_dot(
+                jnp.concatenate([inverse[index], residual[index]], axis=0), residual[index]
+            )
+            inverse[index] += both[:block]
+            residual[index] = both[block:]
         return limit * limit, trips + 1
 
     lax.while_loop(
@@ -340,50 +569,61 @@
         (bound * bound, jnp.int32(0)),
     )
 
-    def correct(index, carry):
-        guess = inverse[...]
-        residual[...] = identity - guess - exact_dot(gram, guess)
-        inverse[...] = guess + exact_dot(guess, residual[...])
+    def correct(trip, carry):
+        for index in range(problems):
+            guess = inverse[index]
+            residual[index] = identity - guess - exact_dot(gram_of(coupling[index]), guess)
+            inverse[index] = guess + exact_dot(guess, residual[index])
         return carry
 
-    lax.fori_loop(0, jnp.where(spread > 32.0, 4, 0), correct, 0)
-    upper = exact_dot(inverse[...], turn)
-    lower = exact_dot(turn, upper, 0)
-    parts = (
-        (0, 0, 2.0 * inverse[...] - identity),
-        (0, 1, 2.0 * upper),
-        (1, 0, -2.0 * upper.T),
-        (1, 1, identity - 2.0 * lower),
-    )
-    for down, across, value in parts:
-        high, low = split(value)
-        where = (pl.ds(down * block, block), pl.ds(across * block, block))
-        rot_high[where] = high
-        rot_low[where] = low
-
-
-def rotation_of(total, rows_all):
-    block = 2 * total.shape[2]
+    lax.fori_loop(0, jnp.where(spread_most > 32.0, 4, 0), correct, 0)
+    for index in range(problems):
+        turn = coupling[index]
+        upper = exact_dot(inverse[index], turn)
+        lower = exact_dot(turn, upper, 0)
+        left = (2.0 * inverse[index] - identity, -2.0 * upper.T)
+        right = (2.0 * upper, identity - 2.0 * lower)
+        for down in range(2):
+            place = pl.ds(down * block, block)
+            if index == 0:
+                value = jnp.concatenate([left[down], right[down]], axis=1)
+            else:
+                odd = lax.rem(lax.axis_index("pairs"), 2) == 1
+                value = jnp.where(odd, right[down], left[down])
+            high, low = split(value)
+            outs[2 * index][place, :] = high
+            outs[2 * index + 1][place, :] = low
+
+
+def rotation_of(rows_all, *totals):
+    block = 2 * totals[0].shape[2]
+    problems = len(totals)
     vmem = pl.BlockSpec(memory_space=pltpu.VMEM)
+    outs = [jax.ShapeDtypeStruct((2 * block, 2 * block), BF16)] * 2
+    if problems > 1:
+        outs += [jax.ShapeDtypeStruct((2 * block, block), BF16)] * 2
     return pl.pallas_call(
-        functools.partial(rotation_kernel, rows_all),
-        out_shape=[jax.ShapeDtypeStruct((2 * block, 2 * block), BF16)] * 2,
-        in_specs=[vmem],
-        out_specs=[vmem, vmem],
-        scratch_shapes=[pltpu.VMEM((block, block), F32)] * 3,
+        functools.partial(rotation_kernel, rows_all, problems),
+        out_shape=outs,
+        in_specs=[vmem] * problems,
+        out_specs=[vmem] * len(outs),
+        scratch_shapes=[pltpu.VMEM((problems, block, block), F32)] * 3,
         name="rotation",
         compiler_params=pltpu.CompilerParams(vmem_limit_bytes=32 * 2**20),
-    )(total)
+    )(*totals)
 
 
 def shards(matrix):
     rows_all = matrix.shape[0] * lax.axis_size("rows")
     (total,) = stage("products", 0, matrix, None, True)
-    for turn_index in range(STEPS - 1):
-        rotation = rotation_of(total, rows_all)
-        matrix, total = stage("turn_and_products", 1, matrix, rotation, True)
-    rotation = rotation_of(total, rows_all)
-    (matrix,) = stage("last_turn", 2, matrix, rotation, False)
+    rotation = rotation_of(rows_all, total)
+    matrix, total, kept, extra, total_near = stage(
+        "turn_and_products", 1, matrix, rotation, True, True
+    )
+    high, low, near_high, near_low = rotation_of(rows_all, total, total_near)
+    (matrix,) = stage(
+        "last_turn", 2, matrix, (high, low), False, True, (kept, extra, near_high, near_low)
+    )
     return matrix
 
 

time: 109 us -> 111 us (1.018)
  Pallas kernels: 104 us -> 106 us
    pallas_call x5, Pallas kernels: 104 us -> 106 us  [the longest x3 89.5 us: stage(): pl.pallas_call(functools.partial(stage_kernel, rotates, sums, ahead, coun...]
where the time goes in v2:
time: 111 us
  Pallas kernels  106 us (95%)
  local copies, waits for them, and re-layouts  4.64 us (4%)
    pallas_call x3, Pallas kernels, stage(): pl.pallas_call(functools.partial(stage_kernel, rotates, sums, ahead, coun...  89.5 us
    pallas_call x2, Pallas kernels, rotation_of(): pl.pallas_call(functools.partial(rotation_kernel, rows_all, problems), ou...  16.3 us
    unnamed x1, local copies, waits for them, and re-layouts  4.64 us

profile of v2, /device:TPU:1, one launch (start us, length us, event | category | flops | bytes accessed | tf_op | source)
XLA Modules:
  0.0 110.5 jit_solution(12901866801884338612)
XLA Ops:
  0.0 20.1 %products.1.refs_0_ = f32[8,80,128]{2,1,0:T(8,128)S(1)} custom-call(f32[2048,512]{1,0:T(8,128)} %refs_0_.3), custom_call_target="tpu_custom_call" | custom-call | tf_op jit(solution)/shard_map/products/pallas_call | solution.py:502
  20.1 5.6 %rotation.2 = (bf16[512,512]{1,0:T(8,128)(2,1)S(1)}, bf16[512,512]{1,0:T(8,128)(2,1)S(1)}) custom-call(f32[8,80,128]{2,1,0:T(8,128)S(1)} %products.1.refs_0_), custom_call_target="tpu_custom_call" | custom-call | tf_op jit(solution)/shard_map/rotation/pallas_call | solution.py:605
  25.6 56.6 %turn_and_products.1 = (f32[2048,512]{1,0:T(8,128)}, f32[8,80,128]{2,1,0:T(8,128)S(1)}, f32[2048,256]{1,0:T(8,128)S(1)}, f32[2048,256]{1,0:T(8,128)}, f32[8,80,128]{2,1,0:T(8,128)S(1)}) custom-call(f32[2048,512]{1,0:T(8,128)} %refs_0_.3, bf16[512,512]{1,0:T(8,128)(2,1)S(1)} %get-tuple-element.16.refs_1_, bf16[512,512]{1,0:T(8,128)(2,1)S(1)} %get-tuple-element.17.refs_2_), custom_call_target="tpu_custom_call" | custom-call | tf_op jit(solution)/shard_map/turn_and_products/pallas_call | solution.py:502
  82.2 10.7 %rotation.3 = (bf16[512,512]{1,0:T(8,128)(2,1)S(1)}, bf16[512,512]{1,0:T(8,128)(2,1)S(1)}, bf16[512,256]{1,0:T(8,128)(2,1)S(1)}, bf16[512,256]{1,0:T(8,128)(2,1)S(1)}) custom-call(f32[8,80,128]{2,1,0:T(8,128)S(1)} %get-tuple-element.19.refs_0_, f32[8,80,128]{2,1,0:T(8,128)S(1)} %get-tuple-element.20.refs_1_), custom_call_target="tpu_custom_call" | custom-call | tf_op jit(solution)/shard_map/rotation/pallas_call | solution.py:605
  92.9 12.9 %last_turn.1 = f32[2048,512]{1,0:T(8,128)} custom-call(f32[2048,512]{1,0:T(8,128)} %get-tuple-element.18.refs_0_, bf16[512,512]{1,0:T(8,128)(2,1)S(1)} %get-tuple-element.21.refs_1_, bf16[512,512]{1,0:T(8,128)(2,1)S(1)} %get-tuple-element.22.refs_2_, f32[2048,256]{1,0:T(8,128)S(1)} %get-tuple-element.23.refs_3_, f32[2048,256]{1,0:T(8,128)} %get-tuple-element.24.refs_4_, ...), custom_call_target="tpu_custom_call" | custom-call | tf_op jit(solution)/shard_map/last_turn/pallas_call | solution.py:502
  105.9 4.6 %copy.3 = f32[2048,512]{1,0:T(8,128)} copy(f32[2048,512]{1,0:T(8,128)} %last_turn.1) | data formatting | bytes 8388608

commit v3 on v2

--- a/solution.py
+++ b/solution.py
@@ -8,7 +8,7 @@
 from jax.sharding import PartitionSpec as P
 
 CHUNKS = 8
-LATE = 2
+LATE = 3
 F32 = jnp.float32
 BF16 = jnp.bfloat16
 MESH = pl.DeviceIdType.MESH
@@ -549,15 +549,23 @@
         start = 2.0 / (2.0 + spread)
         first = (1.0 - start) * identity - start * gram
         inverse[index] = start * (identity + first)
-        residual[index] = exact_dot(first, first)
+        parts = split(first)
+        residual[index] = dot_three(parts, parts, 1)
         spread_most = spread if index == 0 else jnp.maximum(spread_most, spread)
     bound = spread_most / (2.0 + spread_most)
 
     def grow(state):
         limit, trips = state
         for index in range(problems):
-            both = exact_dot(
-                jnp.concatenate([inverse[index], residual[index]], axis=0), residual[index]
+            high, low = split(residual[index])
+            inverse_high, inverse_low = split(inverse[index])
+            both = dot_three(
+                (
+                    jnp.concatenate([inverse_high, high], axis=0),
+                    jnp.concatenate([inverse_low, low], axis=0),
+                ),
+                (high, low),
+                1,
             )
             inverse[index] += both[:block]
             residual[index] = both[block:]
@@ -613,6 +621,23 @@
     )(*totals)
 
 
+def copy_kernel(source, target):
+    target[...] = source[...]
+
+
+def written(matrix):
+    rows, cols = matrix.shape
+    spec = pl.BlockSpec((rows // CHUNKS, cols), lambda chunk: (chunk, 0))
+    return pl.pallas_call(
+        copy_kernel,
+        out_shape=jax.ShapeDtypeStruct(matrix.shape, matrix.dtype),
+        grid=(CHUNKS,),
+        in_specs=[spec],
+        out_specs=spec,
+        name="written",
+    )(matrix)
+
+
 def shards(matrix):
     rows_all = matrix.shape[0] * lax.axis_size("rows")
     (total,) = stage("products", 0, matrix, None, True)
@@ -624,7 +649,7 @@
     (matrix,) = stage(
         "last_turn", 2, matrix, (high, low), False, True, (kept, extra, near_high, near_low)
     )
-    return matrix
+    return written(matrix)
 
 
 def solution(mesh):

time: 111 us -> 111 us (level)
  local copies, waits for them, and re-layouts: 4.64 us -> 0 us
  Pallas kernels: 106 us -> 110 us
    pallas_call x0 -> x1, Pallas kernels: none -> 6.59 us  [written(): pl.pallas_call(copy_kernel, out_shape=jax.ShapeDtypeStruct(matrix.shape,...]
    pallas_call x2, Pallas kernels: 16.3 us -> 11.6 us  [rotation_of(): pl.pallas_call(functools.partial(rotation_kernel, rows_all, problems), ou...]
    unnamed x1 -> x0, local copies, waits for them, and re-layouts: 4.64 us -> none
    pallas_call x3, Pallas kernels: 89.5 us -> 92.1 us  [stage(): pl.pallas_call(functools.partial(stage_kernel, rotates, sums, ahead, coun...]
where the time goes in v3:
time: 111 us; the launch traced here: 110 us
  Pallas kernels  110 us (99%)
    pallas_call x3, Pallas kernels, stage(): pl.pallas_call(functools.partial(stage_kernel, rotates, sums, ahead, coun...  92.1 us
    pallas_call x2, Pallas kernels, rotation_of(): pl.pallas_call(functools.partial(rotation_kernel, rows_all, problems), ou...  11.6 us
    pallas_call x1, Pallas kernels, written(): pl.pallas_call(copy_kernel, out_shape=jax.ShapeDtypeStruct(matrix.shape,...  6.59 us

profile of v3, /device:TPU:1, one launch (start us, length us, event | category | flops | bytes accessed | tf_op | source)
XLA Modules:
  0.0 110.3 jit_solution(17551165593283670221)
XLA Ops:
  0.0 20.1 %products.1.refs_0_ = f32[8,80,128]{2,1,0:T(8,128)S(1)} custom-call(f32[2048,512]{1,0:T(8,128)} %refs_0_.3), custom_call_target="tpu_custom_call" | custom-call | tf_op jit(solution)/shard_map/products/pallas_call | solution.py:502
  20.1 4.2 %rotation.2 = (bf16[512,512]{1,0:T(8,128)(2,1)S(1)}, bf16[512,512]{1,0:T(8,128)(2,1)S(1)}) custom-call(f32[8,80,128]{2,1,0:T(8,128)S(1)} %products.1.refs_0_), custom_call_target="tpu_custom_call" | custom-call | tf_op jit(solution)/shard_map/rotation/pallas_call | solution.py:613
  24.3 55.7 %turn_and_products.1 = (f32[2048,512]{1,0:T(8,128)}, f32[8,80,128]{2,1,0:T(8,128)S(1)}, f32[2048,256]{1,0:T(8,128)S(1)}, f32[2048,256]{1,0:T(8,128)}, f32[8,80,128]{2,1,0:T(8,128)S(1)}) custom-call(f32[2048,512]{1,0:T(8,128)} %refs_0_.3, bf16[512,512]{1,0:T(8,128)(2,1)S(1)} %get-tuple-element.16.refs_1_, bf16[512,512]{1,0:T(8,128)(2,1)S(1)} %get-tuple-element.17.refs_2_), custom_call_target="tpu_custom_call" | custom-call | tf_op jit(solution)/shard_map/turn_and_products/pallas_call | solution.py:502
  80.0 7.3 %rotation.3 = (bf16[512,512]{1,0:T(8,128)(2,1)S(1)}, bf16[512,512]{1,0:T(8,128)(2,1)S(1)}, bf16[512,256]{1,0:T(8,128)(2,1)S(1)}, bf16[512,256]{1,0:T(8,128)(2,1)S(1)}) custom-call(f32[8,80,128]{2,1,0:T(8,128)S(1)} %get-tuple-element.19.refs_0_, f32[8,80,128]{2,1,0:T(8,128)S(1)} %get-tuple-element.20.refs_1_), custom_call_target="tpu_custom_call" | custom-call | tf_op jit(solution)/shard_map/rotation/pallas_call | solution.py:613
  87.4 16.3 %last_turn.1.source = f32[2048,512]{1,0:T(8,128)} custom-call(f32[2048,512]{1,0:T(8,128)} %get-tuple-element.18.refs_0_, bf16[512,512]{1,0:T(8,128)(2,1)S(1)} %get-tuple-element.21.refs_1_, bf16[512,512]{1,0:T(8,128)(2,1)S(1)} %get-tuple-element.22.refs_2_, f32[2048,256]{1,0:T(8,128)S(1)} %get-tuple-element.23.refs_3_, ...), custom_call_target="tpu_custom_call" | custom-call | tf_op jit(solution)/shard_map/last_turn/pallas_call | solution.py:502
  103.7 6.6 %written.1 = f32[2048,512]{1,0:T(8,128)} custom-call(f32[2048,512]{1,0:T(8,128)} %last_turn.1.source), custom_call_target="tpu_custom_call" | custom-call | tf_op jit(solution)/shard_map/written/pallas_call | solution.py:631
